TPU v7x, 256 devices: a whole 4x4x8 slice. The times are simulated.
256 devices in a mesh: seq: 2 (over core), vocab: 128 (over y, z, x).
Axes of the slice: x: 4, y: 4, z: 8, core: 2. Of those that a mesh axis runs over, the one named last changes fastest.
Arguments:
- hidden: bfloat16 [1024, 8192], P('seq', 'vocab'), may hold values from -80 to 80
- weight: bfloat16 [8192, 65536], P('seq', 'vocab'), may hold values from -0.06629126 to 0.06629126, as said below
- tangent: bfloat16 [8192, 65536], P('seq', 'vocab'), may hold values from -0.0625 to 0.0625
- targets: int32 [1024], P('seq'), may hold values from 0 to 65535
Outputs:
- ggn: bfloat16 [8192, 65536], P('seq', 'vocab')
- token_loss: float32 [1024], P('seq')
Inputs may be any that keep to these rules, and one draw needn't show every extreme that they name: `weight`: entries of standard deviation about 8192 ** -0.5.
All inputs are finite; a program needn't handle non-finite values.
Results may differ from a plain program's by a relative error of at most 0.0065.
Values may be sent and summed in bfloat16 or wider, within the bound.
A program may use at most 64 MiB of HBM per device.

v0:
```python
import jax
import jax.numpy as jnp
from jax import lax
from jax.sharding import Mesh
from jax.sharding import PartitionSpec as P

VOCAB = ("vocab_0", "vocab_1", "vocab_2")


def partner(value, axis, stride):
    mask = 2**stride
    pairs = [(source, source ^ mask) for source in range(lax.axis_size(axis))]
    return lax.ppermute(value, axis, pairs)


def split_up(shard, dim, count):
    lengths = shard.shape
    parts = shard.reshape(*lengths[:dim], count, lengths[dim] // count, *lengths[dim + 1 :])
    return jnp.moveaxis(parts, dim, 0)


def sent_and_summed(shard, axis, dim):
    count = lax.axis_size(axis)
    parts = lax.all_to_all(split_up(shard, dim, count), axis, 0, 0, tiled=True)
    return jnp.sum(parts, axis=0)


def sent_together(arrays, axis, dim, along):
    widths = [a.shape[along] for a in arrays]
    both = jnp.concatenate(arrays, axis=along)
    whole = sent_and_summed(both, axis, dim)
    return tuple(jnp.split(whole, [sum(widths[:k]) for k in range(1, len(widths))], axis=along))


def all_in_one(shard, axis):
    leaves = jax.tree.leaves(shard)
    turns = sorted(range(len(leaves)), key=lambda k: -leaves[k].size)
    width = (1, *leaves[turns[0]].shape)[-1]
    lines = [
        jnp.pad(leaves[k].reshape(-1), (0, -leaves[k].size % width)).reshape(-1, width)
        for k in turns
    ]
    both, at, found = (lax.all_gather(jnp.concatenate(lines), axis), 0, {})
    for k, line in zip(turns, lines):
        piece = both[:, at : at + len(line)].reshape(len(both), -1)
        found[k] = piece[:, : leaves[k].size].reshape(-1, *leaves[k].shape)
        at += len(line)
    numbers = iter(range(len(leaves)))
    return jax.tree.map(lambda _: found[next(numbers)], shard)


def joined_all(shard, axes, combine):
    for axis in axes:
        pieces = all_in_one(shard, axis)
        shard = jax.tree.map(lambda part: part[0], pieces)
        for k in range(1, lax.axis_size(axis)):
            shard = combine(shard, jax.tree.map(lambda part: part[k], pieces))
    return shard


def combine_rows(earlier, later):
    row_top = jnp.maximum(earlier[0], later[0])
    scale_a = jnp.exp(earlier[0] - row_top)
    scale_b = jnp.exp(later[0] - row_top)
    return (
        row_top,
        earlier[1] * scale_a + later[1] * scale_b,
        earlier[2] * scale_a + later[2] * scale_b,
        earlier[3] + later[3],
    )


def on_device(hidden, weight, tangent, targets):
    vocab_index = lax.axis_index(VOCAB)
    shard_width = weight.shape[1]
    half_width = weight.shape[0]
    whole = lax.all_gather(hidden, VOCAB, axis=1, tiled=True)
    seq_index = lax.axis_index("seq")
    own_part = lax.dynamic_slice_in_dim(whole, seq_index * half_width, half_width, 1)
    far_part = lax.dynamic_slice_in_dim(whole, (1 - seq_index) * half_width, half_width, 1)
    received = partner(far_part, "seq", 0)
    leading = jnp.where(seq_index == 0, own_part, received)
    trailing = jnp.where(seq_index == 0, received, own_part)
    stacked = jnp.concatenate([leading, trailing], axis=0)
    partial_logits = jnp.dot(stacked, weight, preferred_element_type=jnp.float32)
    partial_tangent = jnp.dot(stacked, tangent, preferred_element_type=jnp.float32)
    logits, tangent_logits = sent_together((partial_logits, partial_tangent), "seq", 0, 1)
    local_target = targets - vocab_index * shard_width
    columns_ids = jnp.arange(shard_width, dtype=jnp.int32)
    picked_local = jnp.sum(
        jnp.where(columns_ids[None, :] == local_target[:, None], logits, jnp.float32(0.0)), axis=1
    )
    local_top = jnp.max(logits, axis=1)
    local_exp = jnp.exp(logits - local_top[:, None])
    row_top, totals, tangent_sum, picked = joined_all(
        (
            local_top,
            jnp.sum(local_exp, axis=1),
            jnp.sum(local_exp * tangent_logits, axis=1),
            picked_local,
        ),
        VOCAB,
        combine_rows,
    )
    exp_logits = jnp.exp(logits - row_top[:, None])
    expect = tangent_sum / totals
    token_loss = row_top + jnp.log(totals) - picked
    weight_term = (exp_logits / totals[:, None] * (tangent_logits - expect[:, None])).astype(
        jnp.bfloat16
    )
    far_term = partner(weight_term, "seq", 0)
    lead_term = jnp.where(seq_index == 0, weight_term, far_term)
    trail_term = jnp.where(seq_index == 0, far_term, weight_term)
    all_terms = jnp.concatenate([lead_term, trail_term], axis=0)
    ggn = jnp.einsum("td,tv->dv", stacked, all_terms, preferred_element_type=jnp.float32).astype(
        jnp.bfloat16
    )
    return (ggn, token_loss)


def solution(mesh):
    split = Mesh(
        mesh.devices.reshape(mesh.shape["seq"], 4, 8, 4), ("seq", "vocab_0", "vocab_1", "vocab_2")
    )
    placed = (P("seq", VOCAB), P("seq", VOCAB), P("seq", VOCAB), P("seq"))
    return jax.shard_map(
        on_device,
        mesh=split,
        in_specs=placed,
        out_specs=(P("seq", VOCAB), P("seq")),
        check_vma=False,
    )
```

profile of v0, /device:TPU:1, one launch (start us, length us, event | category | flops | bytes accessed | tf_op | source)
XLA Modules:
  0.0 243.7 jit_solution(8856782322527806862)
XLA Ops:
  7.2 0.0 all-gather.8.cloned.1.call-start
  7.2 0.7 all-gather.8.cloned.1.call-update
  7.9 0.0 copy-start.4
  7.9 128.0 %all-gather.8.cloned.1.call-done = bf16[512,8192]{0,1:T(8,128)(2,1)} async-done(((bf16[512,64]{0,1:T(8,128)(2,1)}), bf16[512,8192]{0,1:T(8,128)(2,1)}) %all-gather.8.cloned.1.call-update) | async-done | bytes 8388624 | tf_op jit(solution)/shard_map/all_gather | solution.py:77
  136.0 4.5 %constant_dynamic-slice_fusion = bf16[512,4096]{0,1:T(8,128)(2,1)} fusion(bf16[512,8192]{0,1:T(8,128)(2,1)} %all-gather.8.cloned.1.call-done, s32[]{:T(128)S(6)} %select_n.36), kind=kLoop, calls=%fused_computation.174 | loop fusion | bytes 8388612 | tf_op jit(solution)/shard_map/dynamic_slice | solution.py:80
  140.4 4.2 %collective-permute-start = (bf16[512,4096]{0,1:T(8,128)(2,1)}, bf16[512,4096]{0,1:T(8,128)(2,1)}, u32[]{:S(2)}, u32[]{:S(2)}) collective-permute-start(bf16[512,4096]{0,1:T(8,128)(2,1)} %constant_dynamic-slice_fusion), channel_id=1, source_target_pairs={{0,128},{128,0},{1,129},{129,1},{2,130},{130,2},{3,131},{131,3},{4... | collective-permute-start | bytes 12582920 | tf_op jit(solution)/shard_map/ppermute | solution.py:13
  144.6 0.0 copy-done.4
  144.6 0.0 copy-start.5
  144.6 7.1 %collective-permute-done = bf16[512,4096]{0,1:T(8,128)(2,1)} collective-permute-done((bf16[512,4096]{0,1:T(8,128)(2,1)}, bf16[512,4096]{0,1:T(8,128)(2,1)}, u32[]{:S(2)}, u32[]{:S(2)}) %collective-permute-start) | collective-permute-done | bytes 4194336 | tf_op jit(solution)/shard_map/ppermute | solution.py:13
  151.7 4.3 %broadcast_select_fusion.1 = (bf16[512,4096]{0,1:T(8,128)(2,1)S(1)}, bf16[512,4096]{0,1:T(8,128)(2,1)S(1)}) fusion(bf16[512,4096]{0,1:T(8,128)(2,1)} %collective-permute-done, pred[]{:T(512)S(6)} %eq.8, bf16[512,8192]{0,1:T(8,128)(2,1)} %all-gather.8.cloned.1.call-done, s32[]{:T(128)S(6)} %select_n.35), kind=kLoop, calls=%fused_computation.5 | loop fusion | flops 4194304 | bytes 16777220 | tf_op jit(solution)/shard_map/jit(_where)/select_n | solution.py:82
  156.0 0.0 copy-start
  156.0 0.0 copy-start.2
  156.1 0.0 copy-done.5
  156.1 0.0 copy-start.6
  156.1 4.5 %fusion.1 = f32[1024,512]{0,1:T(8,128)S(1)} fusion(bf16[4096,512]{1,0:T(8,128)(2,1)S(1)} %copy-done.5, bf16[512,4096]{0,1:T(8,128)(2,1)S(1)} %get-tuple-element.17, bf16[512,4096]{0,1:T(8,128)(2,1)S(1)} %get-tuple-element.16), kind=kOutput, calls=%fused_computation.7 | convolution fusion | flops 4311744512 | bytes 14680064 | tf_op jit(solution)/shard_map/dot_general | solution.py:85
  160.6 0.0 copy-done
  160.6 0.0 copy-done.2
  160.6 0.5 copy-done.6
  161.2 4.5 %fusion = f32[1024,512]{0,1:T(8,128)S(1)} fusion(bf16[4096,512]{1,0:T(8,128)(2,1)S(1)} %copy-done.6, bf16[512,4096]{0,1:T(8,128)(2,1)S(1)} %get-tuple-element.17, bf16[512,4096]{0,1:T(8,128)(2,1)S(1)} %get-tuple-element.16), kind=kOutput, calls=%fused_computation.6 | convolution fusion | flops 4311744512 | bytes 14680064 | tf_op jit(solution)/shard_map/dot_general | solution.py:86
  165.7 0.5 pad_maximum_fusion.1
  166.2 0.5 copy.13
  166.7 8.2 %all_to_all.5 = f32[2,512,1024]{1,2,0:T(8,128)} all-to-all(f32[2,512,1024]{1,2,0:T(8,128)S(1)} %bitcast.422), channel_id=1, replica_groups=mesh['seq'=2,'vocab_0'=4,'vocab_1'=8,'vocab_2'=4] {'seq'}, dimensions={0} | all-to-all | bytes 8388608 | tf_op jit(solution)/shard_map/all_to_all | solution.py:24
  174.9 2.9 %reduce_sum.36 = f32[512,1024]{0,1:T(8,128)S(1)} reduce(f32[2,512,1024]{1,2,0:T(8,128)} %all_to_all.5, f32[]{:T(128)} %constant.12.clone.1), dimensions={0}, to_apply=%region_0.1 | reduce | flops 524288 | bytes 6291460 | tf_op jit(solution)/shard_map/reduce_sum | solution.py:25
  177.8 0.1 slice_reduce_fusion
  177.9 0.0 copy-start.1
  177.9 0.0 copy-start.3
  177.9 0.3 fusion.5
  178.2 9.5 %all-gather.3 = f32[4,4,512]{2,1,0:T(4,128)S(1)} all-gather(f32[1,4,512]{2,1,0:T(4,128)S(1)} %maximum_bitcast_fusion), channel_id=2, replica_groups=mesh['seq'=2,'vocab_0'=4,'vocab_1'=8,'vocab_2'=4] {'vocab_0'}, dimensions={0}, use_global_device_ids=true | all-gather | bytes 40960 | tf_op jit(solution)/shard_map/all_gather | solution.py:43
  187.8 18.5 %all-gather.4 = f32[8,4,512]{2,1,0:T(4,128)S(1)} all-gather(f32[1,4,512]{2,1,0:T(4,128)S(1)} %maximum_bitcast_fusion.1), channel_id=3, replica_groups=mesh['seq'=2,'vocab_0'=4,'vocab_1'=8,'vocab_2'=4] {'vocab_1'}, dimensions={0}, use_global_device_ids=true | all-gather | bytes 73728 | tf_op jit(solution)/shard_map/all_gather | solution.py:43
  206.4 0.1 fusion.29
  206.5 0.1 fusion.8
  206.5 9.0 %all-gather.5 = f32[4,4,512]{2,1,0:T(4,128)S(1)} all-gather(f32[1,4,512]{2,1,0:T(4,128)S(1)} %maximum_bitcast_fusion.2), channel_id=4, replica_groups=mesh['seq'=2,'vocab_0'=4,'vocab_1'=8,'vocab_2'=4] {'vocab_2'}, dimensions={0}, use_global_device_ids=true | all-gather | bytes 40960 | tf_op jit(solution)/shard_map/all_gather | solution.py:43
  215.6 0.6 add_subtract_fusion
  216.2 0.3 multiply_convert_fusion
  216.5 12.2 %collective-permute-start.1 = (bf16[512,512]{0,1:T(8,128)(2,1)S(1)}, bf16[512,512]{0,1:T(8,128)(2,1)S(1)}, u32[]{:S(2)}, u32[]{:S(2)}) collective-permute-start(bf16[512,512]{0,1:T(8,128)(2,1)S(1)} %multiply_convert_fusion), channel_id=1, source_target_pairs={{0,128},{128,0},{1,129},{129,1},{2,130},{130,2},{3,131},{131,3},{4... | collective-permute-start | bytes 1572872 | tf_op jit(solution)/shard_map/ppermute | solution.py:13
  228.8 1.5 collective-permute-done.1
  230.3 0.4 broadcast_select_fusion.3
  230.7 0.0 copy-done.1
  230.7 0.0 copy-done.3
  230.7 6.1 %convolution_convert_fusion = bf16[4096,512]{1,0:T(8,128)(2,1)} fusion(bf16[512,4096]{0,1:T(8,128)(2,1)S(1)} %copy-done.3, bf16[512,4096]{0,1:T(8,128)(2,1)S(1)} %copy-done.1, bf16[512,512]{0,1:T(8,128)(2,1)S(1)} %get-tuple-element.19, bf16[512,512]{0,1:T(8,128)(2,1)S(1)} %get-tuple-element.18), kind=kOutput, calls=%fused_computation.1 | convolution fusion | flops 4315938816 | bytes 13631488 | tf_op jit(solution)/shard_map/td,tv->dv/dot_general | solution.py:115
  (10 shorter events, 0.2 us)
Async XLA Ops:
  7.2 128.8 %all-gather.8.cloned.1.call-start = ((), (), s32[]{:S(2)}) async-start(), calls=%async_computation.1 | async-start | bytes 8454144 | tf_op jit(solution)/shard_map/all_gather | solution.py:77
  7.9 136.7 %copy-start.4 = (s32[512]{0:T(512)S(1)}, s32[512]{0:T(512)}, u32[]{:S(2)}) copy-start(s32[512]{0:T(512)} %param.7) | copy-start | bytes 6148
  140.4 11.3 %collective-permute-start = (bf16[512,4096]{0,1:T(8,128)(2,1)}, bf16[512,4096]{0,1:T(8,128)(2,1)}, u32[]{:S(2)}, u32[]{:S(2)}) collective-permute-start(bf16[512,4096]{0,1:T(8,128)(2,1)} %constant_dynamic-slice_fusion), channel_id=1, source_target_pairs={{0,128},{128,0},{1,129},{129,1},{2,130},{130,2},{3,131},{131,3},{4... | collective-permute-start | bytes 12582920 | tf_op jit(solution)/shard_map/ppermute | solution.py:13
  144.6 11.4 %copy-start.5 = (bf16[4096,512]{1,0:T(8,128)(2,1)S(1)}, bf16[4096,512]{1,0:T(8,128)(2,1)}, u32[]{:S(2)}) copy-start(bf16[4096,512]{1,0:T(8,128)(2,1)} %param.5) | copy-start | bytes 12582916
  156.0 4.6 %copy-start = (bf16[512,4096]{0,1:T(8,128)(2,1)}, bf16[512,4096]{0,1:T(8,128)(2,1)S(1)}, u32[]{:S(2)}) copy-start(bf16[512,4096]{0,1:T(8,128)(2,1)S(1)} %get-tuple-element.16) | copy-start | bytes 12582916
  156.0 4.6 %copy-start.2 = (bf16[512,4096]{0,1:T(8,128)(2,1)}, bf16[512,4096]{0,1:T(8,128)(2,1)S(1)}, u32[]{:S(2)}) copy-start(bf16[512,4096]{0,1:T(8,128)(2,1)S(1)} %get-tuple-element.17) | copy-start | bytes 12582916
  156.1 5.1 %copy-start.6 = (bf16[4096,512]{1,0:T(8,128)(2,1)S(1)}, bf16[4096,512]{1,0:T(8,128)(2,1)}, u32[]{:S(2)}) copy-start(bf16[4096,512]{1,0:T(8,128)(2,1)} %param.6) | copy-start | bytes 12582916
  177.9 52.8 %copy-start.1 = (bf16[512,4096]{0,1:T(8,128)(2,1)S(1)}, bf16[512,4096]{0,1:T(8,128)(2,1)}, u32[]{:S(2)}) copy-start(bf16[512,4096]{0,1:T(8,128)(2,1)} %copy-done) | copy-start | bytes 12582916
  177.9 52.8 %copy-start.3 = (bf16[512,4096]{0,1:T(8,128)(2,1)S(1)}, bf16[512,4096]{0,1:T(8,128)(2,1)}, u32[]{:S(2)}) copy-start(bf16[512,4096]{0,1:T(8,128)(2,1)} %copy-done.2) | copy-start | bytes 12582916
  216.5 13.8 %collective-permute-start.1 = (bf16[512,512]{0,1:T(8,128)(2,1)S(1)}, bf16[512,512]{0,1:T(8,128)(2,1)S(1)}, u32[]{:S(2)}, u32[]{:S(2)}) collective-permute-start(bf16[512,512]{0,1:T(8,128)(2,1)S(1)} %multiply_convert_fusion), channel_id=1, source_target_pairs={{0,128},{128,0},{1,129},{129,1},{2,130},{130,2},{3,131},{131,3},{4... | collective-permute-start | bytes 1572872 | tf_op jit(solution)/shard_map/ppermute | solution.py:13
Sparse Core Ops, SparseCore 0:
  11.6 124.3 all-gather.7
where the time goes:
time: 244 us
  waiting for transfers between devices  137 us (56%)
  blocking collectives  45.3 us (19%)
  starting transfers between devices  16.5 us (7%)
  matrix products  15.2 us (6%)
  between operations  14.2 us (6%)
  other arithmetic  9.69 us (4%)
  local copies, waits for them, and re-layouts  5.47 us (2%)
    all_gather x1, waiting for transfers between devices, on_device(): whole = lax.all_gather(hidden, VOCAB, axis=1, tiled=True)  128 us
    all_gather x3, blocking collectives, all_in_one(): both, at, found = (lax.all_gather(jnp.concatenate(lines), axis), 0, {})  37.1 us
    ppermute x2, starting transfers between devices, partner(): return lax.ppermute(value, axis, pairs)  16.4 us
    ppermute x2, waiting for transfers between devices, partner(): return lax.ppermute(value, axis, pairs)  8.66 us
    all_to_all x1, blocking collectives, sent_and_summed(): parts = lax.all_to_all(split_up(shard, dim, count), axis, 0, 0, tiled=True)  8.21 us
    dot_general x1, matrix products, on_device(): jnp.einsum('td,tv->dv', stacked, all_terms, preferred_element_type=jnp.fl...  6.1 us
  transfers between devices with their start and end apart: 3, of which 3 were waited for; matrix products, arithmetic and copies ran while one was open for 0% of the time, Pallas kernels for 0%

commit v1 on v0

v1 whole, which is shorter than its diff:
```python
import functools

import jax
import jax.numpy as jnp
from jax import lax
from jax.experimental import pallas as pl
from jax.experimental.pallas import tpu as pltpu
from jax.sharding import Mesh
from jax.sharding import PartitionSpec as P

VOCAB = ("vocab_0", "vocab_1", "vocab_2")
MESH = pl.DeviceIdType.MESH
F32, BF16 = jnp.float32, jnp.bfloat16
GROUPS, LANES, ROWS, WIDTH, HALF = 4, 128, 64, 512, 4096
CUTS = ((16, 32), (16, 48), (16, 32), (32, 48))
PLANE, LINE_Z, RING_Z, FAR_Z, LINE_Y, RING_X, FAR_X, LINE_X, RING_Y, FAR_Y = range(10)
ORDER = (
    (0, 0), (1, 0), (0, 1), (0, 2), (1, 1), (0, 3), (5, 0, 0, -1), (2, 0, 1, -1), (5, 0, 0, 1), (8, 0, 0, -1), (8, 0,
    0, 1), (4, 0, 3), (7, 0, 3), (1, 2), (2, 1, 1, -1), (4, 0, 1), (8, 1, 0, -1), (4, 0, 2), (5, 1, 0, -1), (2, 2, 1,
    -1), (8, 1, 0, 1), (7, 0, 2), (4, 1, 3), (7, 1, 3), (2, 0, 1, 1), (1, 3), (7, 0, 1), (5, 0, 3, -1), (2, 1, 1, 1),
    (5, 2, 0, -1), (5, 1, 0, 1), (8, 0, 3, -1), (2, 3, 1, -1), (4, 1, 2), (6, 0, 0), (7, 2, 3), (2, 2, 1, 1), (9, 0,
    0), (4, 1, 1), (8, 2, 0, -1), (2, 0, 2, -1), (5, 0, 1, -1), (7, 1, 1), (4, 2, 3), (7, 1, 2), (2, 1, 2, -1), (8, 1,
    3, -1), (5, 0, 2, -1), (5, 0, 3, 1), (8, 0, 3, 1), (2, 3, 1, 1), (5, 2, 0, 1), (2, 2, 2, -1), (8, 0, 2, -1), (5,
    1, 3, -1), (9, 1, 0), (8, 3, 0, -1), (5, 3, 0, -1), (2, 0, 2, 1), (8, 2, 0, 1), (4, 3, 3), (7, 3, 3), (2, 1, 2,
    1), (4, 2, 1), (7, 2, 2), (8, 0, 1, -1), (4, 2, 2), (2, 3, 2, -1), (7, 2, 1), (5, 1, 2, -1), (2, 2, 2, 1), (8, 1,
    3, 1), (5, 0, 1, 1), (5, 2, 3, -1), (2, 0, 3, -1), (6, 1, 0), (5, 0, 2, 1), (8, 0, 2, 1), (2, 1, 3, -1), (8, 2, 3,
    -1), (5, 1, 1, -1), (8, 3, 0, 1), (8, 1, 1, -1), (2, 3, 2, 1), (5, 1, 3, 1), (2, 2, 3, -1), (8, 1, 2, -1), (5, 3,
    0, 1), (6, 2, 0), (4, 3, 1), (2, 0, 3, 1), (5, 3, 3, -1), (4, 3, 2), (5, 2, 1, -1), (6, 0, 3), (9, 0, 3), (7, 3,
    1), (2, 3, 3, -1), (9, 2, 0), (5, 2, 2, -1), (8, 3, 3, -1), (2, 1, 3, 1), (8, 0, 1, 1), (7, 3, 2), (2, 2, 3, 1),
    (8, 2, 3, 1), (6, 0, 2), (8, 2, 2, -1), (5, 1, 2, 1), (8, 1, 1, 1), (5, 2, 3, 1), (8, 1, 2, 1), (5, 3, 1, -1), (6,
    0, 1), (6, 1, 3), (8, 2, 1, -1), (9, 3, 0), (5, 3, 2, -1), (9, 1, 3), (6, 3, 0), (2, 3, 3, 1), (5, 1, 1, 1), (3,
    0), (3, 1), (9, 0, 2), (8, 3, 3, 1), (9, 0, 1), (5, 3, 3, 1), (8, 3, 1, -1), (6, 1, 2), (5, 2, 1, 1), (3, 2), (8,
    2, 2, 1), (6, 1, 1), (6, 2, 3), (8, 3, 2, -1), (5, 2, 2, 1), (9, 1, 1), (8, 2, 1, 1), (9, 2, 3), (9, 3, 3), (9, 1,
    2), (5, 3, 1, 1), (8, 3, 1, 1), (6, 3, 3), (5, 3, 2, 1), (6, 2, 1), (3, 3), (6, 2, 2), (8, 3, 2, 1), (9, 2, 2),
    (6, 3, 2), (9, 2, 1), (6, 3, 1), (9, 3, 2), (9, 3, 1),
)


class Gather:
    def __init__(self, block, held, lent, send_sems, recv_sems, far_sems):
        self.block, self.held, self.lent = block, held, lent
        self.send_sems, self.recv_sems, self.far_sems = send_sems, recv_sems, far_sems
        self.core, self.y, self.z, self.x = (lax.axis_index(a) for a in ("seq",) + VOCAB)
        self.names, self.far_names, self.sent, self.begun = {}, {}, 0, []
        self.left = {}
        for kind, group, *_ in ORDER:
            part = self.part(kind)
            self.left[group, part] = self.left.get((group, part), 0) + 1

    @staticmethod
    def part(kind):
        if kind in (PLANE, RING_Z, FAR_Z):
            return 0
        return 1 if kind in (LINE_Y, RING_X, FAR_X) else 2

    def rows(self, group, part):
        ends = (0, *CUTS[group], ROWS)
        return pl.ds(ends[part], ends[part + 1] - ends[part])

    def near(self, axis, step):
        at, count = {"y": (self.y, 4), "z": (self.z, 8), "x": (self.x, 4)}[axis]
        return lax.rem(at + step + count, count)

    def chip(self, **steps):
        return (self.core, *(self.near(a, steps.get(a, 0)) for a in "yzx"))

    def arrival(self, *name):
        if name not in self.names:
            self.names[name] = len(self.names)
        return self.recv_sems.at[self.names[name]]

    def departure(self):
        self.sent += 1
        return self.send_sems.at[self.sent - 1]

    def send(self, source, target, name, device, departure=None):
        copy = pltpu.make_async_remote_copy(
            src_ref=source,
            dst_ref=target,
            send_sem=self.departure() if departure is None else departure,
            recv_sem=self.arrival(*name),
            device_id=device,
            device_id_type=MESH,
        )
        copy.start()
        if departure is None:
            self.begun.append(copy)

    def take(self, ref, *name):
        pltpu.make_async_copy(ref, ref, self.arrival(*name)).wait()

    def ring(self, ref, axis, kind, group, piece, steps=(1, -1)):
        for step in steps:
            self.send(ref, ref, (kind, group, piece, step), self.chip(**{axis: step}))

    def start(self):
        self.lines = []
        for group in range(GROUPS):
            rest = pl.ds(CUTS[group][0], ROWS - CUTS[group][0])
            source = self.block.at[group, rest]
            target = self.held.at[group, self.y, self.z, self.x, rest]
            sem = self.departure()
            for step in (4, 3, 5, 2, 6, 1, 7):
                self.send(source, target, (LINE_Z, group), self.chip(z=step), sem)
            pltpu.make_async_copy(source, target, self.arrival(LINE_Z, group)).start()
            self.lines.append((self.held.at[group, 0, 0:7, 0, rest], sem))
            first = self.rows(group, 0)
            source = self.block.at[group, first]
            target = self.held.at[group, self.y, self.z, self.x, first]
            sem = self.departure()
            for dy in (2, 1, 3, 0):
                for dx in (2, 1, 3, 0):
                    if dy or dx:
                        self.send(source, target, (PLANE, group), self.chip(y=dy, x=dx), sem)
            pltpu.make_async_copy(source, target, self.arrival(PLANE, group)).start()
            self.lines.append((self.held.at[group, 0:3, 0:5, 0, first], sem))

    def event(self, kind, group, piece=0, step=0):
        held = self.held
        rows = self.rows(group, self.part(kind))
        if kind == PLANE:
            ref = held.at[group, :, self.z, :, rows]
            self.take(ref, PLANE, group)
            self.ring(ref, "z", RING_Z, group, 1)
        elif kind == LINE_Z:
            rest = pl.ds(CUTS[group][0], ROWS - CUTS[group][0])
            self.take(held.at[group, self.y, :, self.x, rest], LINE_Z, group)
            along_x = held.at[group, self.y, :, self.x, self.rows(group, 1)]
            along_y = held.at[group, self.y, :, self.x, self.rows(group, 2)]
            self.ring(along_y, "y", RING_Y, group, 0)
            self.ring(along_x, "x", RING_X, group, 0)
            for hop in (2, 1, 3):
                self.send(along_y, along_y, (LINE_X, group, hop), self.chip(x=hop))
                self.send(along_x, along_x, (LINE_Y, group, hop), self.chip(y=hop))
        elif kind == RING_Z:
            ref = held.at[group, :, self.near("z", -step * piece), :, rows]
            self.take(ref, RING_Z, group, piece, step)
            if piece < 3:
                self.ring(ref, "z", RING_Z, group, piece + 1, (step,))
            else:
                pl.when(lax.rem(self.core + group, 2) == (0 if step == 1 else 1))(
                    functools.partial(self.far, ref, "z", (FAR_Z, group), step)
                )
        elif kind == FAR_Z:
            self.take(held.at[group, :, self.near("z", 4), :, rows], FAR_Z, group)
        elif kind == LINE_Y:
            ref = held.at[group, self.near("y", -piece), :, self.x, rows]
            self.take(ref, LINE_Y, group, piece)
            self.ring(ref, "x", RING_X, group, piece)
        elif kind == LINE_X:
            ref = held.at[group, self.y, :, self.near("x", -piece), rows]
            self.take(ref, LINE_X, group, piece)
            self.ring(ref, "y", RING_Y, group, piece)
        elif kind == RING_X:
            ref = held.at[group, self.near("y", -piece), :, self.near("x", -step), rows]
            self.take(ref, RING_X, group, piece, step)
            pl.when(lax.rem(self.core + group + piece, 2) == (0 if step == 1 else 1))(
                functools.partial(self.far, ref, "x", (FAR_X, group, piece), step)
            )
        elif kind == RING_Y:
            ref = held.at[group, self.near("y", -step), :, self.near("x", -piece), rows]
            self.take(ref, RING_Y, group, piece, step)
            pl.when(lax.rem(self.core + group + piece, 2) == (0 if step == 1 else 1))(
                functools.partial(self.far, ref, "y", (FAR_Y, group, piece), step)
            )
        elif kind == FAR_X:
            self.take(held.at[group, self.near("y", -piece), :, self.near("x", 2), rows], FAR_X, group, piece)
        elif kind == FAR_Y:
            self.take(held.at[group, self.near("y", 2), :, self.near("x", -piece), rows], FAR_Y, group, piece)
        part = self.part(kind)
        self.left[group, part] -= 1
        if self.left[group, part] == 0:
            self.lend(group, part)

    def far(self, ref, axis, name, step):
        copy = pltpu.make_async_remote_copy(
            src_ref=ref,
            dst_ref=ref,
            send_sem=self.far_sem(name),
            recv_sem=self.arrival(*name),
            device_id=self.chip(**{axis: step}),
            device_id_type=MESH,
        )
        copy.start()

    def far_sem(self, name):
        self.far_names.setdefault(name, len(self.far_names))
        return self.far_sems.at[self.far_names[name]]

    def lend(self, group, part):
        rows = self.rows(group, part)
        source = self.held.at[group, pl.ds(2 - 2 * self.core, 2), :, :, rows]
        target = self.lent.at[group, :, :, :, rows]
        self.send(source, target, ("lend", group, part), (1 - self.core, self.y, self.z, self.x))

    def complete(self, group):
        for part in range(3):
            self.take(self.lent.at[group, :, :, :, self.rows(group, part)], "lend", group, part)

    def finish(self):
        for ref, sem in self.lines:
            pltpu.make_async_copy(ref, ref, sem).wait()
        for copy in self.begun:
            copy.wait_send()
        for (kind, group, *_), at in self.far_names.items():
            rows = self.rows(group, self.part(kind))
            ref = self.held.at[group, :, 0, :, rows] if kind == FAR_Z else self.held.at[group, 0, :, 0, rows]
            pltpu.make_async_copy(ref, ref, self.far_sems.at[at]).wait()


def greet():
    core, y, z, x = (lax.axis_index(a) for a in ("seq",) + VOCAB)
    sem = pltpu.get_barrier_semaphore()

    def plane(i, carry):
        to = (core, lax.rem(y + i // 4, 4), z, lax.rem(x + lax.rem(i, 4), 4))
        pl.semaphore_signal(sem, inc=1, device_id=to, device_id_type=MESH)
        return carry

    def line(i, carry):
        pl.semaphore_signal(sem, inc=1, device_id=(core, y, lax.rem(z + i, 8), x), device_id_type=MESH)
        return carry

    pl.semaphore_signal(sem, inc=1, device_id=(1 - core, y, z, x), device_id_type=MESH)
    lax.fori_loop(1, 8, line, 0)
    lax.fori_loop(1, 16, plane, 0)
    pl.semaphore_wait(sem, 1 + 7 + 15)


def kernel(
    block, targets, weight, tangent, ggn, loss,
    held, lent, staged, turned, near_part, far_part, got_part, plane, line, terms, total, leaving,
    send_sems, recv_sems, far_sems, load_sems, store_sems, part_sems, plane_sems, line_sems, term_sems,
):
    core, y, z, x = (lax.axis_index(a) for a in ("seq",) + VOCAB)
    loads = [
        pltpu.make_async_copy(source, staged.at[k], load_sems.at[k]) for k, source in enumerate((weight, tangent))
    ]
    for copy in loads:
        copy.start()
    greet()
    net = Gather(block, held, lent, send_sems, recv_sems, far_sems)
    net.start()
    partner = (1 - core, y, z, x)
    copies = []

    def turn(first, last):
        def chunk(i, carry):
            k, j = i // 4, lax.rem(i, 4)
            rows = pl.ds(pl.multiple_of(i * 256, 256), 256)
            lanes = pl.ds(pl.multiple_of(j * 256, 256), 256)
            turned[k, 0:WIDTH, lanes] = staged[0, rows, :].T
            turned[k, WIDTH : 2 * WIDTH, lanes] = staged[1, rows, :].T
            return carry

        lax.fori_loop(first, last, chunk, 0)

    def logits(g):
        net.complete(g)
        near_part[g] = jnp.zeros_like(near_part[g])
        far_part[g] = jnp.zeros_like(far_part[g])

        def deep(i, carry):
            half, zs = i // 2, pl.ds(4 * lax.rem(i, 2), 4)
            own = held[g, 2 * core + half, zs].reshape(1024, LANES)
            other = lent[g, half, zs].reshape(1024, LANES)
            product = jnp.dot(turned[i], jnp.concatenate([own, other], axis=1), preferred_element_type=F32)
            near_part[g] += product[:, :LANES]
            far_part[g] += product[:, LANES:]
            return carry

        lax.fori_loop(0, 4, deep, 0)
        copy = pltpu.make_async_remote_copy(
            src_ref=far_part.at[g], dst_ref=got_part.at[g], send_sem=part_sems.at[0, g], recv_sem=part_sems.at[1, g],
            device_id=partner, device_id_type=MESH,
        )
        copy.start()
        copies.append(copy)
        return copy

    def own_stats(g, copy):
        copy.wait_recv()
        values = near_part[g, 0:WIDTH] + got_part[g, 0:WIDTH]
        top = jnp.max(values, axis=0, keepdims=True)
        base = (y * 32 + z * 4 + x) * WIDTH
        ids = lax.broadcasted_iota(jnp.int32, (WIDTH, LANES), 0) + base
        picked = jnp.sum(jnp.where(ids == targets[g : g + 1, :], values, 0.0), axis=0, keepdims=True)
        exps = jnp.exp(values - top)
        near_part[g, 0:WIDTH] = exps
        tangents = near_part[g, WIDTH : 2 * WIDTH] + got_part[g, WIDTH : 2 * WIDTH]
        near_part[g, WIDTH : 2 * WIDTH] = tangents
        plane[g, 0, 0:1, :] = top
        plane[g, 0, 1:2, :] = jnp.sum(exps, axis=0, keepdims=True)
        plane[g, 0, 2:3, :] = jnp.sum(exps * tangents, axis=0, keepdims=True)
        plane[g, 0, 3:4, :] = picked
        plane[g, 0, 4:8, :] = jnp.zeros((4, LANES), F32)

        def give(i, carry):
            pltpu.make_async_remote_copy(
                src_ref=plane.at[g, 0], dst_ref=plane.at[g, i], send_sem=plane_sems.at[0, g],
                recv_sem=plane_sems.at[1, g],
                device_id=(core, lax.rem(y + i // 4, 4), z, lax.rem(x + lax.rem(i, 4), 4)), device_id_type=MESH,
            ).start()
            return carry

        lax.fori_loop(1, 16, give, 0)

    def joined(ref):
        tops = ref[:, 0:1, :]
        top = jnp.max(tops, axis=0)
        scale = jnp.exp(tops - top[None])
        sums = [jnp.sum(ref[:, k : k + 1, :] * scale, axis=0) for k in (1, 2)]
        return top, *sums, jnp.sum(ref[:, 3:4, :], axis=0)

    def plane_stats(g):
        every = plane.at[g, 1:16]
        pltpu.make_async_copy(every, every, plane_sems.at[1, g]).wait()
        for k, row in enumerate(joined(plane.at[g])):
            line[g, 0, k : k + 1, :] = row
        line[g, 0, 4:8, :] = jnp.zeros((4, LANES), F32)

        def give(i, carry):
            pltpu.make_async_remote_copy(
                src_ref=line.at[g, 0], dst_ref=line.at[g, i], send_sem=line_sems.at[0, g],
                recv_sem=line_sems.at[1, g], device_id=(core, y, lax.rem(z + i, 8), x), device_id_type=MESH,
            ).start()
            return carry

        lax.fori_loop(1, 8, give, 0)

    def term(g):
        every = line.at[g, 1:8]
        pltpu.make_async_copy(every, every, line_sems.at[1, g]).wait()
        top, totals, tangent_sum, picked = joined(line.at[g])
        loss[g : g + 1, :] = top + jnp.log(totals) - picked
        scale = jnp.exp(plane[g, 0, 0:1, :] - top) / totals
        expect = tangent_sum / totals
        value = near_part[g, 0:WIDTH] * scale * (near_part[g, WIDTH : 2 * WIDTH] - expect)
        terms[g, 0] = value.T.astype(BF16)
        copy = pltpu.make_async_remote_copy(
            src_ref=terms.at[g, 0], dst_ref=terms.at[g, 1], send_sem=term_sems.at[0, g], recv_sem=term_sems.at[1, g],
            device_id=partner, device_id_type=MESH,
        )
        copy.start()
        copies.append(copy)
        return copy

    def product(i, groups):
        half, zs = i // 4, pl.ds(2 * lax.rem(i, 4), 2)
        left, right = [], []
        for g in groups:
            left += [held[g, 2 * core + half, zs].reshape(512, LANES), lent[g, half, zs].reshape(512, LANES)]
            right += [terms[g, 0], terms[g, 1]]
        left, right = jnp.concatenate(left, axis=1), jnp.concatenate(right, axis=0)
        return jnp.dot(left, right, preferred_element_type=F32)

    def early(i, carry):
        total[pl.ds(pl.multiple_of(i * 512, 512), 512)] = product(i, (0, 1, 2))
        return carry

    def last(i, carry):
        rows = pl.ds(pl.multiple_of(i * 512, 512), 512)
        slot = lax.rem(i, 2)
        out = pltpu.make_async_copy(leaving.at[slot], ggn.at[rows], store_sems.at[slot])
        pl.when(i >= 2)(out.wait)
        leaving[slot] = (total[rows] + product(i, (3,))).astype(BF16)
        out.start()
        return carry

    for copy in loads:
        copy.wait()
    turns = {0: (0, 4), 1: (4, 8), 2: (8, 12), 6: (12, 16)}
    parts, sent = {}, {}
    ready = 0
    for at, event in enumerate(ORDER):
        if at in turns:
            turn(*turns[at])
        net.event(*event)
        while ready < GROUPS and not any(net.left[ready, p] for p in range(3)):
            g = ready
            parts[g] = logits(g)
            if g >= 1:
                own_stats(g - 1, parts[g - 1])
            if g >= 2:
                plane_stats(g - 2)
            if g >= 3:
                sent[g - 3] = term(g - 3)
            ready += 1
    own_stats(3, parts[3])
    plane_stats(2)
    sent[1] = term(1)
    plane_stats(3)
    sent[2] = term(2)
    for g in range(3):
        sent[g].wait_recv()
    lax.fori_loop(0, 8, early, 0)
    sent[3] = term(3)
    sent[3].wait_recv()
    lax.fori_loop(0, 8, last, 0)
    for slot in range(2):
        pltpu.make_async_copy(leaving.at[slot], ggn.at[0:512], store_sems.at[slot]).wait()
    net.finish()
    for copy in copies:
        copy.wait_send()
    for g in range(GROUPS):
        for sems, ref in ((plane_sems, plane.at[g, 1:16]), (line_sems, line.at[g, 1:8])):
            pltpu.make_async_copy(ref, ref, sems.at[0, g]).wait()


def on_device(hidden, weight, tangent, targets):
    block = hidden.reshape(GROUPS, LANES, ROWS).transpose(0, 2, 1)
    vmem, hbm = pl.BlockSpec(memory_space=pltpu.VMEM), pl.BlockSpec(memory_space=pl.ANY)
    dma = pltpu.SemaphoreType.DMA
    ggn, loss = pl.pallas_call(
        kernel,
        out_shape=(
            jax.ShapeDtypeStruct((HALF, WIDTH), BF16),
            jax.ShapeDtypeStruct((GROUPS, LANES), F32),
        ),
        in_specs=[vmem, vmem, hbm, hbm],
        out_specs=(hbm, vmem),
        scratch_shapes=[
            pltpu.VMEM((GROUPS, 4, 8, 4, ROWS, LANES), BF16),
            pltpu.VMEM((GROUPS, 2, 8, 4, ROWS, LANES), BF16),
            pltpu.VMEM((2, HALF, WIDTH), BF16),
            pltpu.VMEM((4, 2 * WIDTH, 1024), BF16),
            pltpu.VMEM((GROUPS, 2 * WIDTH, LANES), F32),
            pltpu.VMEM((GROUPS, 2 * WIDTH, LANES), F32),
            pltpu.VMEM((GROUPS, 2 * WIDTH, LANES), F32),
            pltpu.VMEM((GROUPS, 16, 8, LANES), F32),
            pltpu.VMEM((GROUPS, 8, 8, LANES), F32),
            pltpu.VMEM((GROUPS, 2, LANES, WIDTH), BF16),
            pltpu.VMEM((HALF, WIDTH), F32),
            pltpu.VMEM((2, 512, WIDTH), BF16),
            dma((SENDS,)),
            dma((ARRIVALS,)),
            dma((FARS,)),
            dma((2,)),
            dma((2,)),
            dma((2, GROUPS)),
            dma((2, GROUPS)),
            dma((2, GROUPS)),
            dma((2, GROUPS)),
        ],
        compiler_params=pltpu.CompilerParams(
            collective_id=0, has_side_effects=True, vmem_limit_bytes=60 * 2**20
        ),
        name="head_product",
    )(block, targets.reshape(GROUPS, LANES), weight, tangent)
    return ggn, loss.reshape(-1)


SENDS, ARRIVALS, FARS = 168, 172, 36


def solution(mesh):
    split = Mesh(
        mesh.devices.reshape(mesh.shape["seq"], 4, 8, 4), ("seq", "vocab_0", "vocab_1", "vocab_2")
    )
    placed = (P("seq", VOCAB), P("seq", VOCAB), P("seq", VOCAB), P("seq"))
    return jax.shard_map(
        on_device,
        mesh=split,
        in_specs=placed,
        out_specs=(P("seq", VOCAB), P("seq")),
        check_vma=False,
    )
```

time: 244 us -> 103 us (0.42)
  waiting for transfers between devices: 137 us -> 0 us
  Pallas kernels: 0 us -> 95.3 us
  blocking collectives: 45.3 us -> 0 us
  starting transfers between devices: 16.5 us -> 0 us
  matrix products: 15.2 us -> 0 us
  between operations: 14.2 us -> 0.65 us
  other arithmetic: 9.69 us -> 0 us
    all_gather x1 -> x0, waiting for transfers between devices: 128 us -> none  [on_device(): whole = lax.all_gather(hidden, VOCAB, axis=1, tiled=True)]
    pallas_call x0 -> x1, Pallas kernels: none -> 95.3 us  [on_device(): pl.pallas_call(kernel, out_shape=(jax.ShapeDtypeStruct((HALF, WIDTH), BF1...]
    all_gather x3 -> x0, blocking collectives: 37.1 us -> none  [all_in_one(): both, at, found = (lax.all_gather(jnp.concatenate(lines), axis), 0, {})]
    ppermute x2 -> x0, starting transfers between devices: 16.4 us -> none  [partner(): return lax.ppermute(value, axis, pairs)]
    dot_general x3 -> x0, matrix products: 15.2 us -> none  [the longest x1 6.1 us: on_device(): jnp.einsum('td,tv->dv', stacked, all_terms, preferred_element_type=jnp.fl...]
    ppermute x2 -> x0, waiting for transfers between devices: 8.66 us -> none  [partner(): return lax.ppermute(value, axis, pairs)]
    all_to_all x1 -> x0, blocking collectives: 8.21 us -> none  [sent_and_summed(): parts = lax.all_to_all(split_up(shard, dim, count), axis, 0, 0, tiled=True)]
    unnamed x14 -> x6, local copies, waits for them, and re-layouts: 0.54 us -> 5.89 us
  transfers between devices with their start and end apart: 3 -> 0, of which waited for: 3 -> 0; matrix products, arithmetic and copies ran while one was open for 0% -> 0% of each run, Pallas kernels for 0% -> 0%
where the time goes in v1:
time: 103 us
  Pallas kernels  95.3 us (93%)
  local copies, waits for them, and re-layouts  6.53 us (6%)
    pallas_call x1, Pallas kernels, on_device(): pl.pallas_call(kernel, out_shape=(jax.ShapeDtypeStruct((HALF, WIDTH), BF1...  95.3 us
    unnamed x6, local copies, waits for them, and re-layouts  5.89 us

profile of v1, /device:TPU:1, one launch (start us, length us, event | category | flops | bytes accessed | tf_op | source)
XLA Modules:
  0.0 102.5 jit_solution(10767166484653792497)
XLA Ops:
  0.6 0.0 copy-start
  0.6 0.8 copy-done
  1.5 0.6 bitcast_bitcast_fusion.block
  2.1 95.3 %head_product.1 = (bf16[4096,512]{1,0:T(8,128)(2,1)}, f32[4,128]{1,0:T(4,128)}) custom-call(bf16[4,64,128]{2,1,0:T(8,128)(2,1)} %bitcast_bitcast_fusion.block, s32[4,128]{1,0:T(4,128)} %bitcast.9, bf16[4096,512]{1,0:T(8,128)(2,1)} %weight.1, bf16[4096,512]{1,0:T(8,128)(2,1)} %tangent.1), custom_call_target="tpu_custom_call" | custom-call | tf_op jit(solution)/shard_map/head_product/pallas_call | solution.py:414
  97.4 0.0 copy-start.1
  97.5 4.5 %copy.11 = bf16[4096,512]{1,0:T(8,128)(2,1)} copy(bf16[4096,512]{1,0:T(8,128)(2,1)} %get-tuple-element.8) | data formatting | bytes 8388608
  101.9 0.0 copy-done.1
  101.9 0.6 copy.12
Async XLA Ops:
  0.6 0.8 copy-start
  97.4 4.5 %copy-start.1 = (f32[4,128]{1,0:T(4,128)S(1)}, f32[4,128]{1,0:T(4,128)}, u32[]{:S(2)}) copy-start(f32[4,128]{1,0:T(4,128)} %get-tuple-element.5) | copy-start | bytes 6148

commit v2 on v1

v2 whole, which is shorter than its diff:
```python
import functools
import math

import jax
import jax.numpy as jnp
from jax import lax
from jax.experimental import pallas as pl
from jax.experimental.pallas import tpu as pltpu
from jax.sharding import Mesh
from jax.sharding import PartitionSpec as P

VOCAB = ("vocab_0", "vocab_1", "vocab_2")
MESH = pl.DeviceIdType.MESH
F32, BF16 = jnp.float32, jnp.bfloat16
GROUPS, LANES, ROWS, WIDTH, HALF = 4, 128, 64, 512, 4096
CUTS = ((16, 32), (16, 48), (16, 32), (32, 48))
PLANE, LINE_Z, RING_Z, FAR_Z, LINE_Y, RING_X, FAR_X, LINE_X, RING_Y, FAR_Y, LOGITS = range(11)
ORDER = (
    (0, 0), (1, 0), (0, 1), (0, 2), (1, 1), (4, 0, 3), (7, 0, 3), (0, 3), (8, 0, 0, -1), (5, 0, 0, -1), (2, 0, 1, -1),
    (4, 0, 1), (4, 0, 2), (7, 1, 3), (1, 2), (4, 1, 3), (2, 1, 1, -1), (7, 0, 2), (8, 0, 0, 1), (8, 1, 0, -1), (5, 1,
    0, -1), (7, 0, 1), (2, 2, 1, -1), (5, 0, 3, -1), (1, 3), (8, 0, 3, -1), (5, 0, 0, 1), (2, 0, 1, 1), (5, 0, 1, -1),
    (5, 0, 2, -1), (8, 1, 3, -1), (4, 1, 2), (2, 1, 1, 1), (7, 1, 1), (7, 1, 2), (4, 2, 3), (2, 3, 1, -1), (4, 1, 1),
    (7, 2, 3), (8, 1, 0, 1), (2, 2, 1, 1), (5, 2, 0, -1), (8, 2, 0, -1), (5, 1, 0, 1), (2, 0, 2, -1), (5, 0, 3, 1),
    (8, 0, 3, 1), (5, 1, 3, -1), (8, 0, 2, -1), (5, 0, 1, 1), (2, 1, 2, -1), (8, 1, 3, 1), (5, 0, 2, 1), (2, 3, 1, 1),
    (2, 2, 2, -1), (7, 3, 3), (8, 0, 1, -1), (4, 2, 1), (5, 3, 0, -1), (4, 2, 2), (4, 3, 3), (2, 0, 2, 1), (8, 3, 0,
    -1), (8, 2, 0, 1), (7, 2, 2), (2, 1, 2, 1), (2, 3, 2, -1), (5, 1, 2, -1), (8, 1, 1, -1), (7, 2, 1), (5, 2, 3, -1),
    (8, 0, 2, 1), (2, 2, 2, 1), (8, 1, 2, -1), (5, 2, 0, 1), (2, 0, 3, -1), (5, 1, 1, -1), (8, 2, 3, -1), (5, 1, 3,
    1), (2, 1, 3, -1), (8, 0, 1, 1), (2, 3, 2, 1), (2, 2, 3, -1), (5, 2, 1, -1), (7, 3, 1), (7, 3, 2), (8, 3, 3, -1),
    (4, 3, 1), (5, 3, 3, -1), (4, 3, 2), (2, 0, 3, 1), (5, 3, 0, 1), (5, 2, 2, -1), (8, 3, 0, 1), (8, 1, 1, 1), (2, 1,
    3, 1), (2, 3, 3, -1), (8, 1, 2, 1), (8, 2, 2, -1), (5, 1, 2, 1), (2, 2, 3, 1), (5, 2, 3, 1), (8, 2, 3, 1), (5, 3,
    1, -1), (8, 2, 1, -1), (5, 1, 1, 1), (5, 3, 2, -1), (3, 0), (3, 1), (8, 3, 3, 1), (8, 3, 1, -1), (2, 3, 3, 1), (3,
    2), (6, 0), (8, 3, 2, -1), (5, 2, 1, 1), (10, 0, 0), (5, 3, 3, 1), (3, 3), (8, 2, 2, 1), (5, 2, 2, 1), (10, 1, 0),
    (10, 0, 1), (10, 2, 0), (8, 2, 1, 1), (9, 0), (5, 3, 1, 1), (5, 3, 2, 1), (8, 3, 1, 1), (10, 3, 0), (8, 3, 2, 1),
    (6, 1), (9, 1), (6, 2), (6, 3), (10, 0, 2), (9, 2), (9, 3), (10, 1, 2), (10, 2, 1), (10, 1, 1), (10, 3, 1), (10,
    2, 2), (10, 3, 2),
)


class Gather:
    def __init__(self, block, held, lent, send_sems, recv_sems):
        self.block, self.held, self.lent = block, held, lent
        self.send_sems, self.recv_sems = send_sems, recv_sems
        self.core, self.y, self.z, self.x = (lax.axis_index(a) for a in ("seq",) + VOCAB)
        self.names, self.sent = {}, [0] * GROUPS
        self.left = {}
        for kind, group, *_ in ORDER:
            if kind == LOGITS:
                continue
            part = self.part(kind)
            self.left[group, part] = self.left.get((group, part), 0) + 1

    @staticmethod
    def part(kind):
        if kind in (PLANE, RING_Z, FAR_Z):
            return 0
        return 1 if kind in (LINE_Y, RING_X, FAR_X) else 2

    def rows(self, group, part):
        ends = (0, *CUTS[group], ROWS)
        return pl.ds(ends[part], ends[part + 1] - ends[part])

    def near(self, axis, step):
        at, count = {"y": (self.y, 4), "z": (self.z, 8), "x": (self.x, 4)}[axis]
        return lax.rem(at + step + count, count)

    def chip(self, **steps):
        return (self.core, *(self.near(a, steps.get(a, 0)) for a in "yzx"))

    def arrival(self, *name):
        if name not in self.names:
            self.names[name] = len(self.names)
        return self.recv_sems.at[self.names[name]]

    def send(self, source, target, name, device, cond=None, counted=True):
        group = name[1]
        copy = pltpu.make_async_remote_copy(
            src_ref=source,
            dst_ref=target,
            send_sem=self.send_sems.at[group],
            recv_sem=self.arrival(*name),
            device_id=device,
            device_id_type=MESH,
        )
        if counted:
            self.sent[group] += math.prod(target.shape[:-1])
        if cond is None:
            copy.start()
        else:
            pl.when(cond)(copy.start)

    def take(self, ref, *name):
        pltpu.make_async_copy(ref, ref, self.arrival(*name)).wait()

    def ring(self, ref, axis, kind, group, piece, steps=(1, -1)):
        for step in steps:
            self.send(ref, ref, (kind, group, piece, step), self.chip(**{axis: step}))

    def start(self):
        for group in range(GROUPS):
            lanes = pl.ds(group * LANES, LANES)
            rest = pl.ds(CUTS[group][0], ROWS - CUTS[group][0])
            source = self.block.at[rest, lanes]
            target = self.held.at[group, self.y, self.z, self.x, rest]
            for step in (4, 3, 5, 2, 6, 1, 7):
                self.send(source, target, (LINE_Z, group), self.chip(z=step))
            pltpu.make_async_copy(source, target, self.arrival(LINE_Z, group)).start()
            first = self.rows(group, 0)
            source = self.block.at[first, lanes]
            target = self.held.at[group, self.y, self.z, self.x, first]
            for dy in (2, 1, 3, 0):
                for dx in (2, 1, 3, 0):
                    if dy or dx:
                        self.send(source, target, (PLANE, group), self.chip(y=dy, x=dx))
            pltpu.make_async_copy(source, target, self.arrival(PLANE, group)).start()

    def event(self, kind, group, piece=0, step=0):
        held = self.held
        rows = self.rows(group, self.part(kind))
        if kind == PLANE:
            ref = held.at[group, :, self.z, :, rows]
            self.take(ref, PLANE, group)
            self.ring(ref, "z", RING_Z, group, 1)
        elif kind == LINE_Z:
            rest = pl.ds(CUTS[group][0], ROWS - CUTS[group][0])
            self.take(held.at[group, self.y, :, self.x, rest], LINE_Z, group)
            along_x = held.at[group, self.y, :, self.x, self.rows(group, 1)]
            along_y = held.at[group, self.y, :, self.x, self.rows(group, 2)]
            for hop in (2, 1, 3):
                self.send(along_y, along_y, (LINE_X, group, hop), self.chip(x=hop))
                self.send(along_x, along_x, (LINE_Y, group, hop), self.chip(y=hop))
            self.ring(along_y, "y", RING_Y, group, 0)
            self.ring(along_x, "x", RING_X, group, 0)
        elif kind == RING_Z:
            ref = held.at[group, :, self.near("z", -step * piece), :, rows]
            self.take(ref, RING_Z, group, piece, step)
            if piece < 3:
                self.ring(ref, "z", RING_Z, group, piece + 1, (step,))
            else:
                self.far(ref, "z", FAR_Z, group, 0, step)
        elif kind == FAR_Z:
            self.take(held.at[group, :, self.near("z", 4), :, rows], FAR_Z, group)
        elif kind == LINE_Y:
            ref = held.at[group, self.near("y", -piece), :, self.x, rows]
            self.take(ref, LINE_Y, group, piece)
            self.ring(ref, "x", RING_X, group, piece)
        elif kind == LINE_X:
            ref = held.at[group, self.y, :, self.near("x", -piece), rows]
            self.take(ref, LINE_X, group, piece)
            self.ring(ref, "y", RING_Y, group, piece)
        elif kind == RING_X:
            ref = held.at[group, self.near("y", -piece), :, self.near("x", -step), rows]
            self.take(ref, RING_X, group, piece, step)
            self.far(ref, "x", FAR_X, group, piece, step)
        elif kind == RING_Y:
            ref = held.at[group, self.near("y", -step), :, self.near("x", -piece), rows]
            self.take(ref, RING_Y, group, piece, step)
            self.far(ref, "y", FAR_Y, group, piece, step)
        elif kind == FAR_X:
            self.take(held.at[group, :, :, self.near("x", 2), rows], FAR_X, group)
        elif kind == FAR_Y:
            self.take(held.at[group, self.near("y", 2), :, :, rows], FAR_Y, group)
        part = self.part(kind)
        self.left[group, part] -= 1
        if self.left[group, part] == 0:
            self.lend(group, part)

    def far(self, ref, axis, kind, group, piece, step):
        this_way = lax.rem(self.core + group + piece, 2) == (0 if step == 1 else 1)
        self.send(ref, ref, (kind, group), self.chip(**{axis: step}), this_way, step == 1)

    def lend(self, group, part):
        rows = self.rows(group, part)
        source = self.held.at[group, pl.ds(2 - 2 * self.core, 2), :, :, rows]
        target = self.lent.at[group, :, :, :, rows]
        self.send(source, target, ("lend", group, part), (1 - self.core, self.y, self.z, self.x))

    def finish(self, ref):
        for group, lines in enumerate(self.sent):
            every = ref.at[0 : lines * LANES * 2 // (WIDTH * 4)]
            pltpu.make_async_copy(every, every, self.send_sems.at[group]).wait()


def greet():
    core, y, z, x = (lax.axis_index(a) for a in ("seq",) + VOCAB)
    sem = pltpu.get_barrier_semaphore()

    def plane(i, carry):
        to = (core, lax.rem(y + i // 4, 4), z, lax.rem(x + lax.rem(i, 4), 4))
        pl.semaphore_signal(sem, inc=1, device_id=to, device_id_type=MESH)
        return carry

    def line(i, carry):
        pl.semaphore_signal(sem, inc=1, device_id=(core, y, lax.rem(z + i, 8), x), device_id_type=MESH)
        return carry

    pl.semaphore_signal(sem, inc=1, device_id=(1 - core, y, z, x), device_id_type=MESH)
    lax.fori_loop(1, 8, line, 0)
    lax.fori_loop(1, 16, plane, 0)
    pl.semaphore_wait(sem, 1 + 7 + 15)


def kernel(
    block, targets, weight, tangent, ggn, loss,
    held, lent, staged, turned, near_part, far_part, got_part, plane, line, terms, total,
    send_sems, recv_sems, load_sems, part_sems, plane_sems, line_sems, term_sems,
):
    core, y, z, x = (lax.axis_index(a) for a in ("seq",) + VOCAB)
    loads = [
        pltpu.make_async_copy(source, staged.at[k], load_sems.at[k]) for k, source in enumerate((weight, tangent))
    ]
    for copy in loads:
        copy.start()
    greet()
    net = Gather(block, held, lent, send_sems, recv_sems)
    net.start()
    partner = (1 - core, y, z, x)
    copies = []

    def turn(first, last):
        def chunk(i, carry):
            tile, at = i // 4, lax.rem(i, 4)
            chips = pl.ds(16 * at, 16)
            rows = pl.ds(pl.multiple_of(tile * 16, 16), 16)
            lanes = pl.ds(pl.multiple_of(at * 256, 256), 256)
            turned[tile, 0:WIDTH, lanes] = staged[0, chips, rows, :].reshape(256, WIDTH).T
            turned[tile, WIDTH : 2 * WIDTH, lanes] = staged[1, chips, rows, :].reshape(256, WIDTH).T
            return carry

        lax.fori_loop(first, last, chunk, 0)

    def logits(g, part):
        net.take(lent.at[g, :, :, :, net.rows(g, part)], "lend", g, part)
        ends = (0, *CUTS[g], ROWS)

        def deep(tile, carry):
            rows = pl.ds(pl.multiple_of(tile * 16, 16), 16)
            own = held[g, pl.ds(2 * core, 2), :, :, rows, :].reshape(1024, LANES)
            other = lent[g, :, :, :, rows, :].reshape(1024, LANES)
            product = jnp.dot(turned[tile], jnp.concatenate([own, other], axis=1), preferred_element_type=F32)
            near_part[g] += product[:, :LANES]
            far_part[g] += product[:, LANES:]
            return carry

        lax.fori_loop(ends[part] // 16, ends[part + 1] // 16 + core // 2, deep, 0)

    def exchange(g):
        copy = pltpu.make_async_remote_copy(
            src_ref=far_part.at[g], dst_ref=got_part.at[g], send_sem=part_sems.at[0, g], recv_sem=part_sems.at[1, g],
            device_id=partner, device_id_type=MESH,
        )
        copy.start()
        copies.append(copy)
        return copy

    def own_stats(g, copy):
        copy.wait_recv()
        values = near_part[g, 0:WIDTH] + got_part[g, 0:WIDTH]
        top = jnp.max(values, axis=0, keepdims=True)
        base = (y * 32 + z * 4 + x) * WIDTH
        ids = lax.broadcasted_iota(jnp.int32, (WIDTH, LANES), 0) + base
        picked = jnp.sum(jnp.where(ids == targets[g : g + 1, :], values, 0.0), axis=0, keepdims=True)
        exps = jnp.exp(values - top)
        near_part[g, 0:WIDTH] = exps
        tangents = near_part[g, WIDTH : 2 * WIDTH] + got_part[g, WIDTH : 2 * WIDTH]
        near_part[g, WIDTH : 2 * WIDTH] = tangents
        plane[g, 0, 0:1, :] = top
        plane[g, 0, 1:2, :] = jnp.sum(exps, axis=0, keepdims=True)
        plane[g, 0, 2:3, :] = jnp.sum(exps * tangents, axis=0, keepdims=True)
        plane[g, 0, 3:4, :] = picked
        plane[g, 0, 4:8, :] = jnp.zeros((4, LANES), F32)

        def give(i, carry):
            pltpu.make_async_remote_copy(
                src_ref=plane.at[g, 0], dst_ref=plane.at[g, i], send_sem=plane_sems.at[0, g],
                recv_sem=plane_sems.at[1, g],
                device_id=(core, lax.rem(y + i // 4, 4), z, lax.rem(x + lax.rem(i, 4), 4)), device_id_type=MESH,
            ).start()
            return carry

        lax.fori_loop(1, 16, give, 0)

    def joined(ref):
        tops = ref[:, 0:1, :]
        top = jnp.max(tops, axis=0)
        scale = jnp.exp(tops - top[None])
        sums = [jnp.sum(ref[:, k : k + 1, :] * scale, axis=0) for k in (1, 2)]
        return top, *sums, jnp.sum(ref[:, 3:4, :], axis=0)

    def plane_stats(g):
        every = plane.at[g, 1:16]
        pltpu.make_async_copy(every, every, plane_sems.at[1, g]).wait()
        for k, row in enumerate(joined(plane.at[g])):
            line[g, 0, k : k + 1, :] = row
        line[g, 0, 4:8, :] = jnp.zeros((4, LANES), F32)

        def give(i, carry):
            pltpu.make_async_remote_copy(
                src_ref=line.at[g, 0], dst_ref=line.at[g, i], send_sem=line_sems.at[0, g],
                recv_sem=line_sems.at[1, g], device_id=(core, y, lax.rem(z + i, 8), x), device_id_type=MESH,
            ).start()
            return carry

        lax.fori_loop(1, 8, give, 0)

    def term(g):
        every = line.at[g, 1:8]
        pltpu.make_async_copy(every, every, line_sems.at[1, g]).wait()
        top, totals, tangent_sum, picked = joined(line.at[g])
        loss[:, g * LANES : (g + 1) * LANES] = top + jnp.log(totals) - picked
        scale = jnp.exp(plane[g, 0, 0:1, :] - top) / totals
        expect = tangent_sum / totals
        value = near_part[g, 0:WIDTH] * scale * (near_part[g, WIDTH : 2 * WIDTH] - expect)
        terms[g, 0] = value.T.astype(BF16)
        copy = pltpu.make_async_remote_copy(
            src_ref=terms.at[g, 0], dst_ref=terms.at[g, 1], send_sem=term_sems.at[0, g], recv_sem=term_sems.at[1, g],
            device_id=partner, device_id_type=MESH,
        )
        copy.start()
        copies.append(copy)
        return copy

    def product(i, groups):
        half, zs = i // 4, pl.ds(2 * lax.rem(i, 4), 2)
        left, right = [], []
        for g in groups:
            left += [held[g, 2 * core + half, zs].reshape(512, LANES), lent[g, half, zs].reshape(512, LANES)]
            right += [terms[g, 0], terms[g, 1]]
        left, right = jnp.concatenate(left, axis=1), jnp.concatenate(right, axis=0)
        return jnp.dot(left, right, preferred_element_type=F32)

    def early(groups, i, carry):
        total[pl.ds(pl.multiple_of(i * 512, 512), 512)] = product(i, groups)
        return carry

    def last(groups, i, carry):
        rows = pl.ds(pl.multiple_of(i * 512, 512), 512)
        ggn[rows] = (total[rows] + product(i, groups)).astype(BF16)
        return carry

    for copy in loads:
        copy.wait()
    near_part[...] = jnp.zeros_like(near_part)
    far_part[...] = jnp.zeros_like(far_part)
    turn(0, 16)
    todo = {g: 3 for g in range(GROUPS)}
    parts, sent, clock = {}, {}, 0.0
    stages = []

    def advance(g, stage):
        nonlocal clock
        clock += 0.5
        if stage == 0:
            own_stats(g, parts[g])
        elif stage == 1:
            plane_stats(g)
        else:
            sent[g] = term(g)
            return
        stages.append((clock + 3.4, g, stage + 1))

    for kind, *rest in ORDER:
        if kind != LOGITS:
            net.event(kind, *rest)
            continue
        while stages and min(stages)[0] <= clock:
            stages.remove(first := min(stages))
            advance(*first[1:])
        logits(*rest)
        g, part = rest
        ends = (0, *CUTS[g], ROWS)
        clock += 0.045 * (ends[part + 1] - ends[part])
        todo[g] -= 1
        if todo[g] == 0:
            parts[g] = exchange(g)
            stages.append((clock + 1.4, g, 0))
    done = ()
    while stages:
        stages.remove(first := min(stages))
        if not done and not stages and first[2] == 2:
            done = tuple(sent)
            for g in done:
                sent[g].wait_recv()
            lax.fori_loop(0, 8, functools.partial(early, done), 0)
            clock += 1.5 * len(done)
        clock = max(clock, first[0])
        advance(*first[1:])
    rest = tuple(g for g in range(GROUPS) if g not in done)
    for g in rest:
        sent[g].wait_recv()
    lax.fori_loop(0, 8, functools.partial(last, rest), 0)
    net.finish(total)
    for copy in copies:
        copy.wait_send()
    for g in range(GROUPS):
        for sems, ref in ((plane_sems, plane.at[g, 1:16]), (line_sems, line.at[g, 1:8])):
            pltpu.make_async_copy(ref, ref, sems.at[0, g]).wait()


def on_device(hidden, weight, tangent, targets):
    block = hidden.T
    weight, tangent = (w.reshape(64, ROWS, WIDTH) for w in (weight, tangent))
    vmem, hbm = pl.BlockSpec(memory_space=pltpu.VMEM), pl.BlockSpec(memory_space=pl.ANY)
    dma = pltpu.SemaphoreType.DMA
    ggn, loss = pl.pallas_call(
        kernel,
        out_shape=(
            pltpu.VMEM((HALF, WIDTH), BF16),
            pltpu.VMEM((1, GROUPS * LANES), F32),
        ),
        in_specs=[vmem, vmem, hbm, hbm],
        out_specs=(vmem, vmem),
        scratch_shapes=[
            pltpu.VMEM((GROUPS, 4, 8, 4, ROWS, LANES), BF16),
            pltpu.VMEM((GROUPS, 2, 8, 4, ROWS, LANES), BF16),
            pltpu.VMEM((2, 64, ROWS, WIDTH), BF16),
            pltpu.VMEM((4, 2 * WIDTH, 1024), BF16),
            pltpu.VMEM((GROUPS, 2 * WIDTH, LANES), F32),
            pltpu.VMEM((GROUPS, 2 * WIDTH, LANES), F32),
            pltpu.VMEM((GROUPS, 2 * WIDTH, LANES), F32),
            pltpu.VMEM((GROUPS, 16, 8, LANES), F32),
            pltpu.VMEM((GROUPS, 8, 8, LANES), F32),
            pltpu.VMEM((GROUPS, 2, LANES, WIDTH), BF16),
            pltpu.VMEM((HALF, WIDTH), F32),
            dma((GROUPS,)),
            dma((ARRIVALS,)),
            dma((2,)),
            dma((2, GROUPS)),
            dma((2, GROUPS)),
            dma((2, GROUPS)),
            dma((2, GROUPS)),
        ],
        compiler_params=pltpu.CompilerParams(
            collective_id=0, has_side_effects=True, vmem_limit_bytes=52 * 2**20
        ),
        name="head_product",
    )(block, targets.reshape(GROUPS, LANES), weight, tangent)
    return ggn, loss.reshape(-1)


ARRIVALS = 144


def solution(mesh):
    split = Mesh(
        mesh.devices.reshape(mesh.shape["seq"], 4, 8, 4), ("seq", "vocab_0", "vocab_1", "vocab_2")
    )
    placed = (P("seq", VOCAB), P("seq", VOCAB), P("seq", VOCAB), P("seq"))
    return jax.shard_map(
        on_device,
        mesh=split,
        in_specs=placed,
        out_specs=(P("seq", VOCAB), P("seq")),
        check_vma=False,
    )
```

time: 103 us -> 88.1 us (0.86)
  Pallas kernels: 95.3 us -> 84.8 us
  local copies, waits for them, and re-layouts: 6.53 us -> 2.59 us
    pallas_call x1, Pallas kernels: 95.3 us -> 84.8 us  [on_device(): pl.pallas_call(kernel, out_shape=(pltpu.VMEM((HALF, WIDTH), BF16), pltpu....]
    unnamed x6 -> x2, local copies, waits for them, and re-layouts: 5.89 us -> 2.59 us
where the time goes in v2:
time: 88.1 us; the launch traced here: 88 us
  Pallas kernels  84.8 us (96%)
  local copies, waits for them, and re-layouts  2.59 us (3%)
    pallas_call x1, Pallas kernels, on_device(): pl.pallas_call(kernel, out_shape=(pltpu.VMEM((HALF, WIDTH), BF16), pltpu....  84.8 us
    unnamed x2, local copies, waits for them, and re-layouts  2.59 us

profile of v2, /device:TPU:1, one launch (start us, length us, event | category | flops | bytes accessed | tf_op | source)
XLA Modules:
  0.0 88.0 jit_solution(16575019852294018135)
XLA Ops:
  0.6 84.8 %head_product.1 = (bf16[4096,512]{1,0:T(8,128)(2,1)S(1)}, f32[1,512]{1,0:T(1,128)S(1)}) custom-call(bf16[64,512]{1,0:T(8,128)(2,1)} %bitcast.8, s32[4,128]{1,0:T(4,128)} %bitcast.9, bf16[64,64,512]{2,1,0:T(8,128)(2,1)} %bitcast.6, bf16[64,64,512]{2,1,0:T(8,128)(2,1)} %bitcast.7), custom_call_target="tpu_custom_call" | custom-call | tf_op jit(solution)/shard_map/head_product/pallas_call | solution.py:404
  85.4 2.0 %copy.8 = bf16[4096,512]{1,0:T(8,128)(2,1)} copy(bf16[4096,512]{1,0:T(8,128)(2,1)S(1)} %get-tuple-element.6) | data formatting | bytes 8388608
  87.4 0.6 copy.9

commit v3 on v2

--- a/solution.py
+++ b/solution.py
@@ -13,26 +13,27 @@
 MESH = pl.DeviceIdType.MESH
 F32, BF16 = jnp.float32, jnp.bfloat16
 GROUPS, LANES, ROWS, WIDTH, HALF = 4, 128, 64, 512, 4096
-CUTS = ((16, 32), (16, 48), (16, 32), (32, 48))
-PLANE, LINE_Z, RING_Z, FAR_Z, LINE_Y, RING_X, FAR_X, LINE_X, RING_Y, FAR_Y, LOGITS = range(11)
+CUTS = ((32, 48), (16, 32), (16, 48), (16, 32))
+PLANE, LINE_Z, RING_Z, FAR_Z, LINE_Y, RING_X, FAR_X, LINE_X, RING_Y, FAR_Y, LOGITS, START, STAGE, EARLY = range(14)
 ORDER = (
-    (0, 0), (1, 0), (0, 1), (0, 2), (1, 1), (4, 0, 3), (7, 0, 3), (0, 3), (8, 0, 0, -1), (5, 0, 0, -1), (2, 0, 1, -1),
-    (4, 0, 1), (4, 0, 2), (7, 1, 3), (1, 2), (4, 1, 3), (2, 1, 1, -1), (7, 0, 2), (8, 0, 0, 1), (8, 1, 0, -1), (5, 1,
-    0, -1), (7, 0, 1), (2, 2, 1, -1), (5, 0, 3, -1), (1, 3), (8, 0, 3, -1), (5, 0, 0, 1), (2, 0, 1, 1), (5, 0, 1, -1),
-    (5, 0, 2, -1), (8, 1, 3, -1), (4, 1, 2), (2, 1, 1, 1), (7, 1, 1), (7, 1, 2), (4, 2, 3), (2, 3, 1, -1), (4, 1, 1),
-    (7, 2, 3), (8, 1, 0, 1), (2, 2, 1, 1), (5, 2, 0, -1), (8, 2, 0, -1), (5, 1, 0, 1), (2, 0, 2, -1), (5, 0, 3, 1),
-    (8, 0, 3, 1), (5, 1, 3, -1), (8, 0, 2, -1), (5, 0, 1, 1), (2, 1, 2, -1), (8, 1, 3, 1), (5, 0, 2, 1), (2, 3, 1, 1),
-    (2, 2, 2, -1), (7, 3, 3), (8, 0, 1, -1), (4, 2, 1), (5, 3, 0, -1), (4, 2, 2), (4, 3, 3), (2, 0, 2, 1), (8, 3, 0,
-    -1), (8, 2, 0, 1), (7, 2, 2), (2, 1, 2, 1), (2, 3, 2, -1), (5, 1, 2, -1), (8, 1, 1, -1), (7, 2, 1), (5, 2, 3, -1),
-    (8, 0, 2, 1), (2, 2, 2, 1), (8, 1, 2, -1), (5, 2, 0, 1), (2, 0, 3, -1), (5, 1, 1, -1), (8, 2, 3, -1), (5, 1, 3,
-    1), (2, 1, 3, -1), (8, 0, 1, 1), (2, 3, 2, 1), (2, 2, 3, -1), (5, 2, 1, -1), (7, 3, 1), (7, 3, 2), (8, 3, 3, -1),
-    (4, 3, 1), (5, 3, 3, -1), (4, 3, 2), (2, 0, 3, 1), (5, 3, 0, 1), (5, 2, 2, -1), (8, 3, 0, 1), (8, 1, 1, 1), (2, 1,
-    3, 1), (2, 3, 3, -1), (8, 1, 2, 1), (8, 2, 2, -1), (5, 1, 2, 1), (2, 2, 3, 1), (5, 2, 3, 1), (8, 2, 3, 1), (5, 3,
-    1, -1), (8, 2, 1, -1), (5, 1, 1, 1), (5, 3, 2, -1), (3, 0), (3, 1), (8, 3, 3, 1), (8, 3, 1, -1), (2, 3, 3, 1), (3,
-    2), (6, 0), (8, 3, 2, -1), (5, 2, 1, 1), (10, 0, 0), (5, 3, 3, 1), (3, 3), (8, 2, 2, 1), (5, 2, 2, 1), (10, 1, 0),
-    (10, 0, 1), (10, 2, 0), (8, 2, 1, 1), (9, 0), (5, 3, 1, 1), (5, 3, 2, 1), (8, 3, 1, 1), (10, 3, 0), (8, 3, 2, 1),
-    (6, 1), (9, 1), (6, 2), (6, 3), (10, 0, 2), (9, 2), (9, 3), (10, 1, 2), (10, 2, 1), (10, 1, 1), (10, 3, 1), (10,
-    2, 2), (10, 3, 2),
+    (0, 0), (1, 0), (1, 1), (0, 1), (4, 0, 3), (7, 0, 3), (8, 0, 0, -1), (5, 0, 0, -1), (7, 0, 1), (4, 0, 1), (4, 1,
+    3), (7, 0, 2), (2, 0, 1, -1), (4, 0, 2), (8, 0, 0, 1), (2, 0, 1, 1), (5, 0, 0, 1), (7, 1, 3), (11, 2), (5, 1, 0,
+    -1), (8, 1, 0, -1), (2, 1, 1, -1), (2, 1, 1, 1), (5, 0, 3, -1), (8, 0, 3, -1), (4, 1, 1), (4, 1, 2), (5, 0, 1,
+    -1), (11, 3), (8, 0, 1, -1), (7, 1, 2), (5, 1, 3, -1), (8, 0, 2, -1), (8, 1, 0, 1), (2, 0, 2, -1), (5, 0, 2, -1),
+    (7, 1, 1), (8, 0, 3, 1), (8, 1, 3, -1), (2, 0, 2, 1), (5, 1, 0, 1), (8, 0, 1, 1), (5, 1, 1, -1), (8, 0, 2, 1), (5,
+    0, 3, 1), (5, 1, 2, -1), (5, 0, 1, 1), (2, 1, 2, -1), (8, 1, 3, 1), (5, 1, 3, 1), (1, 2), (5, 0, 2, 1), (2, 1, 2,
+    1), (8, 1, 2, -1), (8, 1, 1, -1), (5, 1, 1, 1), (7, 2, 3), (0, 2), (2, 0, 3, -1), (5, 1, 2, 1), (8, 1, 2, 1), (5,
+    2, 0, -1), (1, 3), (4, 2, 3), (0, 3), (2, 1, 3, -1), (8, 2, 0, -1), (8, 1, 1, 1), (2, 0, 3, 1), (2, 2, 1, -1), (9,
+    0), (8, 2, 3, -1), (7, 2, 1), (7, 2, 2), (7, 3, 3), (2, 1, 3, 1), (6, 0), (5, 3, 0, -1), (4, 3, 3), (10, 0, 2),
+    (5, 2, 3, -1), (2, 2, 1, 1), (5, 2, 0, 1), (2, 3, 1, -1), (8, 3, 0, -1), (10, 0, 1), (2, 3, 1, 1), (6, 1), (4, 2,
+    2), (3, 1), (3, 0), (5, 3, 3, -1), (8, 2, 1, -1), (2, 2, 2, -1), (4, 2, 1), (8, 2, 2, -1), (8, 2, 0, 1), (8, 3, 3,
+    -1), (8, 2, 3, 1), (2, 3, 2, -1), (7, 3, 2), (2, 2, 2, 1), (10, 1, 1), (10, 1, 0), (7, 3, 1), (5, 2, 2, -1), (10,
+    0, 0), (5, 3, 0, 1), (2, 2, 3, -1), (2, 3, 2, 1), (4, 3, 1), (4, 3, 2), (9, 1), (5, 2, 3, 1), (2, 2, 3, 1), (5, 2,
+    1, -1), (8, 3, 2, -1), (2, 3, 3, -1), (8, 3, 0, 1), (5, 3, 3, 1), (8, 3, 1, -1), (8, 2, 1, 1), (8, 2, 2, 1), (5,
+    2, 2, 1), (5, 3, 1, -1), (2, 3, 3, 1), (5, 3, 2, -1), (10, 1, 2), (12, 0, 0), (3, 2), (8, 3, 3, 1), (5, 2, 1, 1),
+    (5, 3, 1, 1), (5, 3, 2, 1), (3, 3), (8, 3, 2, 1), (8, 3, 1, 1), (10, 2, 0), (6, 2), (10, 3, 0), (12, 1, 0), (6,
+    3), (9, 2), (10, 2, 1), (12, 0, 1), (9, 3), (10, 3, 1), (10, 2, 2), (10, 3, 2), (12, 1, 1), (12, 2, 0), (12, 0,
+    2), (12, 3, 0), (13,), (12, 1, 2), (12, 2, 1), (12, 3, 1), (13,), (12, 2, 2), (12, 3, 2),
 )
 
 
@@ -43,11 +44,10 @@
         self.core, self.y, self.z, self.x = (lax.axis_index(a) for a in ("seq",) + VOCAB)
         self.names, self.sent = {}, [0] * GROUPS
         self.left = {}
-        for kind, group, *_ in ORDER:
-            if kind == LOGITS:
-                continue
-            part = self.part(kind)
-            self.left[group, part] = self.left.get((group, part), 0) + 1
+        for kind, *rest in ORDER:
+            if kind < LOGITS:
+                key = rest[0], self.part(kind)
+                self.left[key] = self.left.get(key, 0) + 1
 
     @staticmethod
     def part(kind):
@@ -95,23 +95,22 @@
         for step in steps:
             self.send(ref, ref, (kind, group, piece, step), self.chip(**{axis: step}))
 
-    def start(self):
-        for group in range(GROUPS):
-            lanes = pl.ds(group * LANES, LANES)
-            rest = pl.ds(CUTS[group][0], ROWS - CUTS[group][0])
-            source = self.block.at[rest, lanes]
-            target = self.held.at[group, self.y, self.z, self.x, rest]
-            for step in (4, 3, 5, 2, 6, 1, 7):
-                self.send(source, target, (LINE_Z, group), self.chip(z=step))
-            pltpu.make_async_copy(source, target, self.arrival(LINE_Z, group)).start()
-            first = self.rows(group, 0)
-            source = self.block.at[first, lanes]
-            target = self.held.at[group, self.y, self.z, self.x, first]
-            for dy in (2, 1, 3, 0):
-                for dx in (2, 1, 3, 0):
-                    if dy or dx:
-                        self.send(source, target, (PLANE, group), self.chip(y=dy, x=dx))
-            pltpu.make_async_copy(source, target, self.arrival(PLANE, group)).start()
+    def start(self, group):
+        lanes = pl.ds(group * LANES, LANES)
+        rest = pl.ds(CUTS[group][0], ROWS - CUTS[group][0])
+        source = self.block.at[rest, lanes]
+        target = self.held.at[group, self.y, self.z, self.x, rest]
+        for step in (4, 3, 5, 2, 6, 1, 7):
+            self.send(source, target, (LINE_Z, group), self.chip(z=step))
+        pltpu.make_async_copy(source, target, self.arrival(LINE_Z, group)).start()
+        first = self.rows(group, 0)
+        source = self.block.at[first, lanes]
+        target = self.held.at[group, self.y, self.z, self.x, first]
+        for dy in (2, 1, 3, 0):
+            for dx in (2, 1, 3, 0):
+                if dy or dx:
+                    self.send(source, target, (PLANE, group), self.chip(y=dy, x=dx))
+        pltpu.make_async_copy(source, target, self.arrival(PLANE, group)).start()
 
     def event(self, kind, group, piece=0, step=0):
         held = self.held
@@ -212,7 +211,9 @@
         copy.start()
     greet()
     net = Gather(block, held, lent, send_sems, recv_sems)
-    net.start()
+    for g in range(GROUPS):
+        if (START, g) not in ORDER:
+            net.start(g)
     partner = (1 - core, y, z, x)
     copies = []
 
@@ -328,8 +329,9 @@
         left, right = jnp.concatenate(left, axis=1), jnp.concatenate(right, axis=0)
         return jnp.dot(left, right, preferred_element_type=F32)
 
-    def early(groups, i, carry):
-        total[pl.ds(pl.multiple_of(i * 512, 512), 512)] = product(i, groups)
+    def early(groups, more, i, carry):
+        rows = pl.ds(pl.multiple_of(i * 512, 512), 512)
+        total[rows] = total[rows] + product(i, groups) if more else product(i, groups)
         return carry
 
     def last(groups, i, carry):
@@ -343,47 +345,31 @@
     far_part[...] = jnp.zeros_like(far_part)
     turn(0, 16)
     todo = {g: 3 for g in range(GROUPS)}
-    parts, sent, clock = {}, {}, 0.0
-    stages = []
-
-    def advance(g, stage):
-        nonlocal clock
-        clock += 0.5
-        if stage == 0:
-            own_stats(g, parts[g])
-        elif stage == 1:
-            plane_stats(g)
+    parts, sent, done = {}, {}, ()
+    for kind, *rest in ORDER:
+        if kind == START:
+            net.start(*rest)
+        elif kind == LOGITS:
+            logits(*rest)
+            todo[rest[0]] -= 1
+            if todo[rest[0]] == 0:
+                parts[rest[0]] = exchange(rest[0])
+        elif kind == STAGE:
+            g, stage = rest
+            if stage == 0:
+                own_stats(g, parts[g])
+            elif stage == 1:
+                plane_stats(g)
+            else:
+                sent[g] = term(g)
+        elif kind == EARLY:
+            some = tuple(g for g in sent if g not in done)
+            for g in some:
+                sent[g].wait_recv()
+            lax.fori_loop(0, 8, functools.partial(early, some, bool(done)), 0)
+            done += some
         else:
-            sent[g] = term(g)
-            return
-        stages.append((clock + 3.4, g, stage + 1))
-
-    for kind, *rest in ORDER:
-        if kind != LOGITS:
             net.event(kind, *rest)
-            continue
-        while stages and min(stages)[0] <= clock:
-            stages.remove(first := min(stages))
-            advance(*first[1:])
-        logits(*rest)
-        g, part = rest
-        ends = (0, *CUTS[g], ROWS)
-        clock += 0.045 * (ends[part + 1] - ends[part])
-        todo[g] -= 1
-        if todo[g] == 0:
-            parts[g] = exchange(g)
-            stages.append((clock + 1.4, g, 0))
-    done = ()
-    while stages:
-        stages.remove(first := min(stages))
-        if not done and not stages and first[2] == 2:
-            done = tuple(sent)
-            for g in done:
-                sent[g].wait_recv()
-            lax.fori_loop(0, 8, functools.partial(early, done), 0)
-            clock += 1.5 * len(done)
-        clock = max(clock, first[0])
-        advance(*first[1:])
     rest = tuple(g for g in range(GROUPS) if g not in done)
     for g in rest:
         sent[g].wait_recv()

time: 88.1 us -> 86.4 us (0.981)
  Pallas kernels: 84.8 us -> 83 us
    pallas_call x1, Pallas kernels: 84.8 us -> 83 us  [on_device(): pl.pallas_call(kernel, out_shape=(pltpu.VMEM((HALF, WIDTH), BF16), pltpu....]
where the time goes in v3:
time: 86.4 us; the launch traced here: 86.3 us
  Pallas kernels  83 us (96%)
  local copies, waits for them, and re-layouts  2.59 us (3%)
    pallas_call x1, Pallas kernels, on_device(): pl.pallas_call(kernel, out_shape=(pltpu.VMEM((HALF, WIDTH), BF16), pltpu....  83 us
    unnamed x2, local copies, waits for them, and re-layouts  2.59 us

profile of v3, /device:TPU:1, one launch (start us, length us, event | category | flops | bytes accessed | tf_op | source)
XLA Modules:
  0.0 86.3 jit_solution(8951350215045117700)
XLA Ops:
  0.6 83.0 %head_product.1 = (bf16[4096,512]{1,0:T(8,128)(2,1)S(1)}, f32[1,512]{1,0:T(1,128)S(1)}) custom-call(bf16[64,512]{1,0:T(8,128)(2,1)} %bitcast.8, s32[4,128]{1,0:T(4,128)} %bitcast.9, bf16[64,64,512]{2,1,0:T(8,128)(2,1)} %bitcast.6, bf16[64,64,512]{2,1,0:T(8,128)(2,1)} %bitcast.7), custom_call_target="tpu_custom_call" | custom-call | tf_op jit(solution)/shard_map/head_product/pallas_call | solution.py:390
  83.7 2.0 %copy.8 = bf16[4096,512]{1,0:T(8,128)(2,1)} copy(bf16[4096,512]{1,0:T(8,128)(2,1)S(1)} %get-tuple-element.6) | data formatting | bytes 8388608
  85.7 0.6 copy.9

commit v4 on v3

--- a/solution.py
+++ b/solution.py
@@ -321,21 +321,21 @@
         return copy
 
     def product(i, groups):
-        half, zs = i // 4, pl.ds(2 * lax.rem(i, 4), 2)
+        half, zs = i // 2, pl.ds(4 * lax.rem(i, 2), 4)
         left, right = [], []
         for g in groups:
-            left += [held[g, 2 * core + half, zs].reshape(512, LANES), lent[g, half, zs].reshape(512, LANES)]
+            left += [held[g, 2 * core + half, zs].reshape(1024, LANES), lent[g, half, zs].reshape(1024, LANES)]
             right += [terms[g, 0], terms[g, 1]]
         left, right = jnp.concatenate(left, axis=1), jnp.concatenate(right, axis=0)
         return jnp.dot(left, right, preferred_element_type=F32)
 
     def early(groups, more, i, carry):
-        rows = pl.ds(pl.multiple_of(i * 512, 512), 512)
+        rows = pl.ds(pl.multiple_of(i * 1024, 1024), 1024)
         total[rows] = total[rows] + product(i, groups) if more else product(i, groups)
         return carry
 
     def last(groups, i, carry):
-        rows = pl.ds(pl.multiple_of(i * 512, 512), 512)
+        rows = pl.ds(pl.multiple_of(i * 1024, 1024), 1024)
         ggn[rows] = (total[rows] + product(i, groups)).astype(BF16)
         return carry
 
@@ -366,14 +366,14 @@
             some = tuple(g for g in sent if g not in done)
             for g in some:
                 sent[g].wait_recv()
-            lax.fori_loop(0, 8, functools.partial(early, some, bool(done)), 0)
+            lax.fori_loop(0, 4, functools.partial(early, some, bool(done)), 0)
             done += some
         else:
             net.event(kind, *rest)
     rest = tuple(g for g in range(GROUPS) if g not in done)
     for g in rest:
         sent[g].wait_recv()
-    lax.fori_loop(0, 8, functools.partial(last, rest), 0)
+    lax.fori_loop(0, 4, functools.partial(last, rest), 0)
     net.finish(total)
     for copy in copies:
         copy.wait_send()

time: 86.4 us -> 85.7 us (level)
  no operation moved by 1% of the time
where the time goes in v4:
time: 85.7 us; the launch traced here: 85.6 us
  Pallas kernels  82.3 us (96%)
  local copies, waits for them, and re-layouts  2.59 us (3%)
    pallas_call x1, Pallas kernels, on_device(): pl.pallas_call(kernel, out_shape=(pltpu.VMEM((HALF, WIDTH), BF16), pltpu....  82.3 us
    unnamed x2, local copies, waits for them, and re-layouts  2.59 us

profile of v4, /device:TPU:1, one launch (start us, length us, event | category | flops | bytes accessed | tf_op | source)
XLA Modules:
  0.0 85.6 jit_solution(15757602152281893535)
XLA Ops:
  0.6 82.3 %head_product.1 = (bf16[4096,512]{1,0:T(8,128)(2,1)S(1)}, f32[1,512]{1,0:T(1,128)S(1)}) custom-call(bf16[64,512]{1,0:T(8,128)(2,1)} %bitcast.8, s32[4,128]{1,0:T(4,128)} %bitcast.9, bf16[64,64,512]{2,1,0:T(8,128)(2,1)} %bitcast.6, bf16[64,64,512]{2,1,0:T(8,128)(2,1)} %bitcast.7), custom_call_target="tpu_custom_call" | custom-call | tf_op jit(solution)/shard_map/head_product/pallas_call | solution.py:390
  83.0 2.0 %copy.8 = bf16[4096,512]{1,0:T(8,128)(2,1)} copy(bf16[4096,512]{1,0:T(8,128)(2,1)S(1)} %get-tuple-element.6) | data formatting | bytes 8388608
  85.0 0.6 copy.9
